TPU v7x, 256 devices: a whole 4x4x8 slice. The times are simulated.
256 devices in a mesh: band: 64 (over y, z, core), feat: 4 (over x).
Axes of the slice: x: 4, y: 4, z: 8, core: 2. Of those that a mesh axis runs over, the one named last changes fastest.
Arguments:
- grid_latent: bfloat16 [131072, 512], P('band', 'feat'), may hold values from -6 to 6
- mesh_latent: bfloat16 [10240, 512], P('band', 'feat'), may hold values from -6 to 6
- edge_latent: bfloat16 [64, 4, 2048, 512], P('band', 'feat'), may hold values from -6 to 6
- edge_src: int32 [64, 8192], P('band'), may hold values from 0 to 2047
- edge_dst: int32 [64, 4, 2048], P('band', 'feat'), may hold values from 0 to 160, as said below
- edge_w1: bfloat16 [1536, 512], replicated, may hold values from -0.15625 to 0.15625
- edge_b1: float32 [512], replicated, may hold values from -3 to 3
- edge_w2: bfloat16 [512, 512], replicated, may hold values from -0.25 to 0.25
- edge_b2: float32 [512], replicated, may hold values from -2 to 2
- edge_gain: float32 [512], replicated, may hold values from 0.25 to 1.75
- edge_shift: float32 [512], replicated, may hold values from -2 to 2
- node_w1: bfloat16 [1024, 512], replicated, may hold values from -0.1875 to 0.1875
- node_b1: float32 [512], replicated, may hold values from -3 to 3
- node_w2: bfloat16 [512, 512], replicated, may hold values from -0.25 to 0.25
- node_b2: float32 [512], replicated, may hold values from -2 to 2
- node_gain: float32 [512], replicated, may hold values from 0.25 to 1.75
- node_shift: float32 [512], replicated, may hold values from -2 to 2
Outputs:
- mesh_new: bfloat16 [10240, 512], P('band', 'feat')
Inputs may be any that keep to these rules, and one draw needn't show every extreme that they name: `edge_src`: entry [s, d * 128 + j] is the grid row, counted within band index s, that sends slot j of the edges from band index s to band index d; empty slots hold some row too. `edge_dst`: entry [d, f, s * 32 + q] is the mesh node, counted within band index d, that receives slot f * 32 + q of the edges from band index s to band index d, or 160 where that slot is empty. The used slots of a pair come first; a pair has at most 128 used slots. Each receiving band index d hears only from the sending band indices of one latitude span of consecutive indices (edges are local), which lies anywhere along band since mesh partitions are face-major; other pairs are empty. In every draw some band indices receive 128 from every band index of their span.
All inputs are finite; a program needn't handle non-finite values.
Results may differ from a plain program's by a relative error of at most 0.011.
Values may be sent and summed in bfloat16 or wider, within the bound.
No kernel may reach another device: no remote copies, remote signals or barrier semaphores. Data moves between devices by JAX's collectives and lax.ppermute only.
A program may use at most 64 MiB of HBM per device.

v0:
```python
import math
import jax
import jax.numpy as jnp
from jax import lax
from jax.sharding import PartitionSpec as P

EPSILON = 1e-05


def cut_along(value, dim, length):
    shape = value.shape
    tiles = value.reshape(*shape[:dim], length, shape[dim] // length, *shape[dim + 1 :])
    return jnp.moveaxis(tiles, dim, 0)


def laid_out(tiles, dim):
    tiles = jnp.moveaxis(tiles, 0, dim)
    shape = tiles.shape
    return tiles.reshape(*shape[:dim], shape[dim] * shape[dim + 1], *shape[dim + 2 :])


def joined_exchange(value, axis, axes, splits, concats):
    sizes = [lax.axis_size(a) for a in axes]
    tiles = cut_along(value, splits[0], sizes[0])
    tiles = jnp.moveaxis(cut_along(tiles, splits[1] + 1, sizes[1]), 0, 1)
    inside = tiles.shape[2:]
    tiles = tiles.reshape(-1, *inside)
    tiles = lax.all_to_all(tiles, axis, split_axis=0, concat_axis=0, tiled=True)
    tiles = laid_out(tiles.reshape(*sizes, *inside), concats[0] + 1)
    return laid_out(tiles, concats[1])


def from_everyone(value, axis):
    length = lax.axis_size(axis)
    return lax.all_to_all(
        jnp.broadcast_to(value[None], (length, *value.shape)), axis, 0, 0, tiled=True
    )


def taken_together(value, axis):
    everything = from_everyone(value, axis)
    return jnp.sum(everything.astype(jnp.float32), axis=0)


def normalize(values, norm_gain, norm_shift):
    average = jnp.mean(values, -1, keepdims=True)
    centered = values - average
    variance = jnp.mean(centered * centered, -1, keepdims=True)
    return centered * lax.rsqrt(variance + EPSILON) * norm_gain + norm_shift


def node_step(row_block, summed, node_w1, node_b1, node_w2, node_b2, node_gain, node_shift):
    full_width = row_block.shape[1]
    hidden = jnp.dot(row_block, node_w1[:full_width], preferred_element_type=jnp.float32)
    hidden = (
        hidden
        + jnp.dot(
            summed.astype(jnp.bfloat16), node_w1[full_width:], preferred_element_type=jnp.float32
        )
        + node_b1
    )
    active = jax.nn.silu(hidden).astype(jnp.bfloat16)
    update = jnp.dot(active, node_w2, preferred_element_type=jnp.float32) + node_b2
    return (row_block.astype(jnp.float32) + normalize(update, node_gain, node_shift)).astype(
        jnp.bfloat16
    )


def select_rows(table, indices):
    total = indices.shape[0]
    block_rows = math.gcd(total, 512)
    grouped = indices.reshape(total // block_rows, block_rows)

    def one_block(block_ids):
        row_ids = lax.broadcasted_iota(jnp.int32, (block_rows, table.shape[0]), 1)
        onehot = (row_ids == block_ids[:, None]).astype(table.dtype)
        return jnp.dot(onehot, table, preferred_element_type=jnp.float32).astype(table.dtype)

    return lax.map(one_block, grouped).reshape(total, table.shape[1])


def body(
    grid_latent,
    mesh_latent,
    edge_latent,
    edge_src,
    edge_dst,
    edge_w1,
    edge_b1,
    edge_w2,
    edge_b2,
    edge_gain,
    edge_shift,
    node_w1,
    node_b1,
    node_w2,
    node_b2,
    node_gain,
    node_shift,
):
    band_count = lax.axis_size("band")
    feat_count = lax.axis_size("feat")
    quarter = grid_latent.shape[1]
    full_width = quarter * feat_count
    mesh_count = mesh_latent.shape[0]
    picked = select_rows(grid_latent, edge_src.reshape(-1)).reshape(band_count, -1, quarter)
    arrived = joined_exchange(picked, ("band", "feat"), ("band", "feat"), (0, 1), (0, 2))
    senders = arrived.reshape(-1, full_width)
    own_edges = edge_latent.reshape(-1, full_width)
    targets = edge_dst.reshape(-1)
    recv_weight = edge_w1[2 * full_width :]
    portion = lax.all_gather(mesh_latent, "feat", axis=1, tiled=True)
    projected = jnp.dot(portion, recv_weight, preferred_element_type=jnp.float32)
    node_ids = lax.broadcasted_iota(jnp.int32, (mesh_count, targets.shape[0]), 0)
    clipped = jnp.minimum(targets, mesh_count - 1)
    pick_node = (node_ids == clipped[None, :]).astype(jnp.float32)
    receiver_part = lax.dot_general(
        pick_node,
        projected,
        (((0,), (0,)), ((), ())),
        precision=lax.Precision.HIGHEST,
        preferred_element_type=jnp.float32,
    )
    hidden = jnp.dot(own_edges, edge_w1[:full_width], preferred_element_type=jnp.float32)
    hidden = hidden + jnp.dot(
        senders, edge_w1[full_width : 2 * full_width], preferred_element_type=jnp.float32
    )
    hidden = hidden + receiver_part + edge_b1
    active = jax.nn.silu(hidden).astype(jnp.bfloat16)
    update = jnp.dot(active, edge_w2, preferred_element_type=jnp.float32) + edge_b2
    edge_new = (own_edges.astype(jnp.float32) + normalize(update, edge_gain, edge_shift)).astype(
        jnp.bfloat16
    )
    selector = (node_ids == targets[None, :]).astype(jnp.bfloat16)
    partial_sums = jnp.dot(selector, edge_new, preferred_element_type=jnp.float32)
    summed = taken_together(partial_sums.astype(jnp.bfloat16), "feat").astype(jnp.float32)
    updated = node_step(portion, summed, node_w1, node_b1, node_w2, node_b2, node_gain, node_shift)
    own_cols = lax.dynamic_slice_in_dim(updated, lax.axis_index("feat") * quarter, quarter, 1)
    return own_cols


def solution(mesh):
    placed = (
        P("band", "feat"),
        P("band", "feat"),
        P("band", "feat", None, None),
        P("band", None),
        P("band", "feat", None),
        P(),
        P(),
        P(),
        P(),
        P(),
        P(),
        P(),
        P(),
        P(),
        P(),
        P(),
        P(),
    )
    return jax.shard_map(
        body, mesh=mesh, in_specs=placed, out_specs=P("band", "feat"), check_vma=False
    )
```

profile of v0, /device:TPU:1, one launch (start us, length us, event | category | flops | bytes accessed | tf_op | source)
XLA Modules:
  0.0 142.4 jit_solution(16497475571590522492)
XLA Ops:
  0.5 1.5 %reduce.4 = s32[8192]{0:T(1024)S(1)} reduce(s32[1,8192]{1,0:T(1,128)} %param.22, s32[]{:T(128)} %broadcast.66), dimensions={0}, to_apply=%param.22.reduce_sub_computation.3 | reduce | bytes 65540 | tf_op args[3]
  2.0 40.9 %while.10 = (s32[]{:T(128)}, bf16[16,512,128]{2,1,0:T(8,128)(2,1)}, s32[16,512]{1,0:T(8,128)S(1)}, bf16[2048,128]{1,0:T(8,128)(2,1)}, s32[]{:T(128)}) while((s32[]{:T(128)}, bf16[16,512,128]{2,1,0:T(8,128)(2,1)}, s32[16,512]{1,0:T(8,128)S(1)}, bf16[2048,128]{1,0:T(8,128)(2,1)}, s32[]{:T(128)}) %tuple.21), condition=%wide.region_1.2_spmd, body=%wide.region_0.1_spmd.sunk | while | flops 269549568 | bytes 662081 | solution.py:79
  2.0 2.5 %fusion.47 = bf16[16,512,128]{2,1,0:T(8,128)(2,1)} fusion(bf16[16,512,128]{2,1,0:T(8,128)(2,1)} %get-tuple-element.73, s32[]{:T(128)} %get-tuple-element.72, bf16[2048,128]{1,0:T(8,128)(2,1)} %get-tuple-element.80, s32[512]{0:T(512)S(1)} %bitcast.42), kind=kOutput, calls=%fused_computation.5.clone.1 | convolution fusion | flops 269549568 | bytes 657920 | tf_op jit(solution)/shard_map/while/body/eval_jaxpr/dot_general | solution.py:77
  4.6 2.5 %fusion.47 = bf16[16,512,128]{2,1,0:T(8,128)(2,1)} fusion(bf16[16,512,128]{2,1,0:T(8,128)(2,1)} %get-tuple-element.73, s32[]{:T(128)} %get-tuple-element.72, bf16[2048,128]{1,0:T(8,128)(2,1)} %get-tuple-element.80, s32[512]{0:T(512)S(1)} %bitcast.42), kind=kOutput, calls=%fused_computation.5.clone.1 | convolution fusion | flops 269549568 | bytes 657920 | tf_op jit(solution)/shard_map/while/body/eval_jaxpr/dot_general | solution.py:77
  7.1 2.5 %fusion.47 = bf16[16,512,128]{2,1,0:T(8,128)(2,1)} fusion(bf16[16,512,128]{2,1,0:T(8,128)(2,1)} %get-tuple-element.73, s32[]{:T(128)} %get-tuple-element.72, bf16[2048,128]{1,0:T(8,128)(2,1)} %get-tuple-element.80, s32[512]{0:T(512)S(1)} %bitcast.42), kind=kOutput, calls=%fused_computation.5.clone.1 | convolution fusion | flops 269549568 | bytes 657920 | tf_op jit(solution)/shard_map/while/body/eval_jaxpr/dot_general | solution.py:77
  9.7 2.6 %fusion.47 = bf16[16,512,128]{2,1,0:T(8,128)(2,1)} fusion(bf16[16,512,128]{2,1,0:T(8,128)(2,1)} %get-tuple-element.73, s32[]{:T(128)} %get-tuple-element.72, bf16[2048,128]{1,0:T(8,128)(2,1)} %get-tuple-element.80, s32[512]{0:T(512)S(1)} %bitcast.42), kind=kOutput, calls=%fused_computation.5.clone.1 | convolution fusion | flops 269549568 | bytes 657920 | tf_op jit(solution)/shard_map/while/body/eval_jaxpr/dot_general | solution.py:77
  12.3 2.5 %fusion.47 = bf16[16,512,128]{2,1,0:T(8,128)(2,1)} fusion(bf16[16,512,128]{2,1,0:T(8,128)(2,1)} %get-tuple-element.73, s32[]{:T(128)} %get-tuple-element.72, bf16[2048,128]{1,0:T(8,128)(2,1)} %get-tuple-element.80, s32[512]{0:T(512)S(1)} %bitcast.42), kind=kOutput, calls=%fused_computation.5.clone.1 | convolution fusion | flops 269549568 | bytes 657920 | tf_op jit(solution)/shard_map/while/body/eval_jaxpr/dot_general | solution.py:77
  14.8 2.5 %fusion.47 = bf16[16,512,128]{2,1,0:T(8,128)(2,1)} fusion(bf16[16,512,128]{2,1,0:T(8,128)(2,1)} %get-tuple-element.73, s32[]{:T(128)} %get-tuple-element.72, bf16[2048,128]{1,0:T(8,128)(2,1)} %get-tuple-element.80, s32[512]{0:T(512)S(1)} %bitcast.42), kind=kOutput, calls=%fused_computation.5.clone.1 | convolution fusion | flops 269549568 | bytes 657920 | tf_op jit(solution)/shard_map/while/body/eval_jaxpr/dot_general | solution.py:77
  17.4 2.5 %fusion.47 = bf16[16,512,128]{2,1,0:T(8,128)(2,1)} fusion(bf16[16,512,128]{2,1,0:T(8,128)(2,1)} %get-tuple-element.73, s32[]{:T(128)} %get-tuple-element.72, bf16[2048,128]{1,0:T(8,128)(2,1)} %get-tuple-element.80, s32[512]{0:T(512)S(1)} %bitcast.42), kind=kOutput, calls=%fused_computation.5.clone.1 | convolution fusion | flops 269549568 | bytes 657920 | tf_op jit(solution)/shard_map/while/body/eval_jaxpr/dot_general | solution.py:77
  19.9 2.5 %fusion.47 = bf16[16,512,128]{2,1,0:T(8,128)(2,1)} fusion(bf16[16,512,128]{2,1,0:T(8,128)(2,1)} %get-tuple-element.73, s32[]{:T(128)} %get-tuple-element.72, bf16[2048,128]{1,0:T(8,128)(2,1)} %get-tuple-element.80, s32[512]{0:T(512)S(1)} %bitcast.42), kind=kOutput, calls=%fused_computation.5.clone.1 | convolution fusion | flops 269549568 | bytes 657920 | tf_op jit(solution)/shard_map/while/body/eval_jaxpr/dot_general | solution.py:77
  22.5 2.5 %fusion.47 = bf16[16,512,128]{2,1,0:T(8,128)(2,1)} fusion(bf16[16,512,128]{2,1,0:T(8,128)(2,1)} %get-tuple-element.73, s32[]{:T(128)} %get-tuple-element.72, bf16[2048,128]{1,0:T(8,128)(2,1)} %get-tuple-element.80, s32[512]{0:T(512)S(1)} %bitcast.42), kind=kOutput, calls=%fused_computation.5.clone.1 | convolution fusion | flops 269549568 | bytes 657920 | tf_op jit(solution)/shard_map/while/body/eval_jaxpr/dot_general | solution.py:77
  25.0 2.5 %fusion.47 = bf16[16,512,128]{2,1,0:T(8,128)(2,1)} fusion(bf16[16,512,128]{2,1,0:T(8,128)(2,1)} %get-tuple-element.73, s32[]{:T(128)} %get-tuple-element.72, bf16[2048,128]{1,0:T(8,128)(2,1)} %get-tuple-element.80, s32[512]{0:T(512)S(1)} %bitcast.42), kind=kOutput, calls=%fused_computation.5.clone.1 | convolution fusion | flops 269549568 | bytes 657920 | tf_op jit(solution)/shard_map/while/body/eval_jaxpr/dot_general | solution.py:77
  27.6 2.5 %fusion.47 = bf16[16,512,128]{2,1,0:T(8,128)(2,1)} fusion(bf16[16,512,128]{2,1,0:T(8,128)(2,1)} %get-tuple-element.73, s32[]{:T(128)} %get-tuple-element.72, bf16[2048,128]{1,0:T(8,128)(2,1)} %get-tuple-element.80, s32[512]{0:T(512)S(1)} %bitcast.42), kind=kOutput, calls=%fused_computation.5.clone.1 | convolution fusion | flops 269549568 | bytes 657920 | tf_op jit(solution)/shard_map/while/body/eval_jaxpr/dot_general | solution.py:77
  30.1 2.5 %fusion.47 = bf16[16,512,128]{2,1,0:T(8,128)(2,1)} fusion(bf16[16,512,128]{2,1,0:T(8,128)(2,1)} %get-tuple-element.73, s32[]{:T(128)} %get-tuple-element.72, bf16[2048,128]{1,0:T(8,128)(2,1)} %get-tuple-element.80, s32[512]{0:T(512)S(1)} %bitcast.42), kind=kOutput, calls=%fused_computation.5.clone.1 | convolution fusion | flops 269549568 | bytes 657920 | tf_op jit(solution)/shard_map/while/body/eval_jaxpr/dot_general | solution.py:77
  32.7 2.5 %fusion.47 = bf16[16,512,128]{2,1,0:T(8,128)(2,1)} fusion(bf16[16,512,128]{2,1,0:T(8,128)(2,1)} %get-tuple-element.73, s32[]{:T(128)} %get-tuple-element.72, bf16[2048,128]{1,0:T(8,128)(2,1)} %get-tuple-element.80, s32[512]{0:T(512)S(1)} %bitcast.42), kind=kOutput, calls=%fused_computation.5.clone.1 | convolution fusion | flops 269549568 | bytes 657920 | tf_op jit(solution)/shard_map/while/body/eval_jaxpr/dot_general | solution.py:77
  35.2 2.5 %fusion.47 = bf16[16,512,128]{2,1,0:T(8,128)(2,1)} fusion(bf16[16,512,128]{2,1,0:T(8,128)(2,1)} %get-tuple-element.73, s32[]{:T(128)} %get-tuple-element.72, bf16[2048,128]{1,0:T(8,128)(2,1)} %get-tuple-element.80, s32[512]{0:T(512)S(1)} %bitcast.42), kind=kOutput, calls=%fused_computation.5.clone.1 | convolution fusion | flops 269549568 | bytes 657920 | tf_op jit(solution)/shard_map/while/body/eval_jaxpr/dot_general | solution.py:77
  37.8 2.5 %fusion.47 = bf16[16,512,128]{2,1,0:T(8,128)(2,1)} fusion(bf16[16,512,128]{2,1,0:T(8,128)(2,1)} %get-tuple-element.73, s32[]{:T(128)} %get-tuple-element.72, bf16[2048,128]{1,0:T(8,128)(2,1)} %get-tuple-element.80, s32[512]{0:T(512)S(1)} %bitcast.42), kind=kOutput, calls=%fused_computation.5.clone.1 | convolution fusion | flops 269549568 | bytes 657920 | tf_op jit(solution)/shard_map/while/body/eval_jaxpr/dot_general | solution.py:77
  40.3 2.5 %fusion.47 = bf16[16,512,128]{2,1,0:T(8,128)(2,1)} fusion(bf16[16,512,128]{2,1,0:T(8,128)(2,1)} %get-tuple-element.73, s32[]{:T(128)} %get-tuple-element.72, bf16[2048,128]{1,0:T(8,128)(2,1)} %get-tuple-element.80, s32[512]{0:T(512)S(1)} %bitcast.42), kind=kOutput, calls=%fused_computation.5.clone.1 | convolution fusion | flops 269549568 | bytes 657920 | tf_op jit(solution)/shard_map/while/body/eval_jaxpr/dot_general | solution.py:77
  42.9 16.6 %all-to-all-start = ((bf16[256,1,32,128]{3,2,1,0:T(8,128)(2,1)}), bf16[256,1,32,128]{3,2,1,0:T(8,128)(2,1)}, u32[]{:S(2)}, u32[]{:S(2)}) async-start(bf16[256,1,32,128]{3,2,1,0:T(8,128)(2,1)} %bitcast.4), calls=%async_computation | async-start | bytes 4194304 | tf_op jit(solution)/shard_map/all_to_all | solution.py:28
  59.5 2.5 %copy.24 = bf16[1,1,2048,512]{2,3,1,0:T(8,128)(2,1)} copy(bf16[1,1,2048,512]{3,2,1,0:T(8,128)(2,1)S(1)} %copy-done.1) | data formatting | bytes 4194304 | tf_op args[2]
  62.0 10.9 %all_gather.3 = bf16[160,512]{1,0:T(8,128)(2,1)S(1)} all-gather(bf16[160,128]{1,0:T(8,128)(2,1)S(1)} %copy-done.5), channel_id=1, replica_groups=mesh['band'=64,'feat'=4] {'feat'}, dimensions={1}, use_global_device_ids=true | all-gather | bytes 204800 | tf_op jit(solution)/shard_map/all_gather | solution.py:112
  72.9 1.3 fusion.16
  74.2 4.2 %fusion.8 = f32[2048,512]{1,0:T(8,128)} fusion(bf16[1,1,2048,512]{3,2,1,0:T(8,128)(2,1)S(1)} %copy-done.1, bf16[1536,512]{1,0:T(8,128)(2,1)} %param.24), kind=kOutput, calls=%fused_computation.14 | convolution fusion | flops 1073741824 | bytes 6815744 | tf_op jit(solution)/shard_map/dot_general | solution.py:124
  78.5 35.0 %all-to-all-done = bf16[256,1,32,128]{3,2,1,0:T(8,128)(2,1)} async-done(((bf16[256,1,32,128]{3,2,1,0:T(8,128)(2,1)}), bf16[256,1,32,128]{3,2,1,0:T(8,128)(2,1)}, u32[]{:S(2)}, u32[]{:S(2)}) %all-to-all-start) | async-done | bytes 2097184 | tf_op jit(solution)/shard_map/all_to_all | solution.py:28
  113.5 2.7 %copy.25 = bf16[64,32,4,128]{3,2,1,0:T(4,128)(2,1)S(1)} copy(bf16[64,32,4,128]{3,1,2,0:T(8,128)(2,1)} %bitcast.8) | data formatting | bytes 4194304 | tf_op jit(solution)/shard_map/transpose | solution.py:17
  116.2 2.4 %fusion.5 = f32[2048,512]{1,0:T(8,128)S(1)} fusion(bf16[256,8,4,128]{3,2,1,0:T(4,128)(2,1)S(1)} %bitcast.41, bf16[1536,512]{1,0:T(8,128)(2,1)} %param.24), kind=kOutput, calls=%fused_computation.11 | convolution fusion | flops 1073741824 | bytes 6815744 | tf_op jit(solution)/shard_map/dot_general | solution.py:125
  118.7 3.0 %multiply_convert_fusion = bf16[2048,512]{1,0:T(8,128)(2,1)S(1)} fusion(f32[2048,512]{1,0:T(8,128)S(1)} %copy-done.2, f32[2048,512]{1,0:T(8,128)S(1)} %fusion.5, f32[160,512]{1,0:T(8,128)S(1)} %fusion.16, f32[512]{0:T(512)S(1)} %copy-done.9, s32[2048]{0:T(1024)S(1)} %broadcast_minimum_fusion), kind=kOutput, calls=%fused_computation.9 | convolution fusion | flops 2021982208 | bytes 10823680 | tf_op jit(solution)/shard_map/dot_general | solution.py:117
  121.7 1.4 add_reduce_fusion
  123.8 0.9 copy-done.3
  124.7 1.6 %fusion.12 = bf16[160,512]{1,0:T(8,128)(2,1)S(1)} fusion(f32[2048,512]{0,1:T(8,128)S(1)} %get-tuple-element.39, bf16[1,1,2048,512]{2,3,1,0:T(8,128)(2,1)S(1)} %copy-done.3, f32[512]{0:T(512)S(1)} %copy-done.10, f32[512]{0:T(512)S(1)} %copy-done.11, f32[2048]{0:T(1024)S(1)} %add_rsqrt_fusion, f32[2048]{0:T(1024)S(1)} %broadcast_multiply_fusion, ...), kind=kOutput, calls=%fused_computation.22 | convolution fusion | flops 344342528 | bytes 6486016 | tf_op jit(solution)/shard_map/dot_general | solution.py:135
  127.2 3.5 %all-to-all-start.1 = ((bf16[4,160,512]{2,1,0:T(8,128)(2,1)}), bf16[4,160,512]{2,1,0:T(8,128)(2,1)S(1)}, u32[]{:S(2)}, u32[]{:S(2)}) async-start(bf16[4,160,512]{2,1,0:T(8,128)(2,1)} %broadcast_in_dim.10), calls=%async_computation.1 | async-start | bytes 1310720 | tf_op jit(solution)/shard_map/all_to_all | solution.py:35
  132.5 8.3 %all-to-all-done.1 = bf16[4,160,512]{2,1,0:T(8,128)(2,1)S(1)} async-done(((bf16[4,160,512]{2,1,0:T(8,128)(2,1)}), bf16[4,160,512]{2,1,0:T(8,128)(2,1)S(1)}, u32[]{:S(2)}, u32[]{:S(2)}) %all-to-all-start.1) | async-done | bytes 655392 | tf_op jit(solution)/shard_map/all_to_all | solution.py:35
  (60 shorter events, 5.6 us)
Async XLA Ops:
  0.0 121.7 %copy-start = (bf16[512,512]{1,0:T(8,128)(2,1)S(1)}, bf16[512,512]{1,0:T(8,128)(2,1)}, u32[]{:S(2)}) copy-start(bf16[512,512]{1,0:T(8,128)(2,1)} %param.26) | copy-start | bytes 1572868
  42.9 16.7 %copy-start.1 = (bf16[1,1,2048,512]{3,2,1,0:T(8,128)(2,1)S(1)}, bf16[1,1,2048,512]{3,2,1,0:T(8,128)(2,1)}, u32[]{:S(2)}) copy-start(bf16[1,1,2048,512]{3,2,1,0:T(8,128)(2,1)} %param.21) | copy-start | bytes 6291460
  42.9 19.2 %copy-start.5 = (bf16[160,128]{1,0:T(8,128)(2,1)S(1)}, bf16[160,128]{1,0:T(8,128)(2,1)}, u32[]{:S(2)}) copy-start(bf16[160,128]{1,0:T(8,128)(2,1)} %param.20) | copy-start | bytes 122884
  42.9 30.1 %copy-start.6 = (s32[1,1,2048]{2,1,0:T(1,128)S(1)}, s32[1,1,2048]{2,1,0:T(1,128)}, u32[]{:S(2)}) copy-start(s32[1,1,2048]{2,1,0:T(1,128)} %param.23) | copy-start | bytes 24580
  42.9 70.6 %all-to-all-start = ((bf16[256,1,32,128]{3,2,1,0:T(8,128)(2,1)}), bf16[256,1,32,128]{3,2,1,0:T(8,128)(2,1)}, u32[]{:S(2)}, u32[]{:S(2)}) async-start(bf16[256,1,32,128]{3,2,1,0:T(8,128)(2,1)} %bitcast.4), calls=%async_computation | async-start | bytes 4194304 | tf_op jit(solution)/shard_map/all_to_all | solution.py:28
  116.2 2.5 %copy-start.2 = (f32[2048,512]{1,0:T(8,128)S(1)}, f32[2048,512]{1,0:T(8,128)}, u32[]{:S(2)}) copy-start(f32[2048,512]{1,0:T(8,128)} %fusion.8) | copy-start | bytes 12582916
  116.2 2.5 %copy-start.9 = (f32[512]{0:T(512)S(1)}, f32[512]{0:T(512)}, u32[]{:S(2)}) copy-start(f32[512]{0:T(512)} %param.25) | copy-start | bytes 6148
  118.6 3.0 %copy-start.7 = (f32[512]{0:T(512)S(1)}, f32[512]{0:T(512)}, u32[]{:S(2)}) copy-start(f32[512]{0:T(512)} %param.27) | copy-start | bytes 6148
  123.1 1.6 %copy-start.3 = (bf16[1,1,2048,512]{2,3,1,0:T(8,128)(2,1)S(1)}, bf16[1,1,2048,512]{2,3,1,0:T(8,128)(2,1)}, u32[]{:S(2)}) copy-start(bf16[1,1,2048,512]{2,3,1,0:T(8,128)(2,1)} %copy.24) | copy-start | bytes 6291460
  123.1 1.6 %copy-start.10 = (f32[512]{0:T(512)S(1)}, f32[512]{0:T(512)}, u32[]{:S(2)}) copy-start(f32[512]{0:T(512)} %param.29) | copy-start | bytes 6148
  123.1 1.6 %copy-start.11 = (f32[512]{0:T(512)S(1)}, f32[512]{0:T(512)}, u32[]{:S(2)}) copy-start(f32[512]{0:T(512)} %param.28) | copy-start | bytes 6148
  124.7 7.6 %copy-start.4 = (bf16[1024,512]{1,0:T(8,128)(2,1)S(1)}, bf16[1024,512]{1,0:T(8,128)(2,1)}, u32[]{:S(2)}) copy-start(bf16[1024,512]{1,0:T(8,128)(2,1)} %param.30) | copy-start | bytes 3145732
  124.7 16.2 %copy-start.8 = (bf16[512,512]{1,0:T(8,128)(2,1)S(1)}, bf16[512,512]{1,0:T(8,128)(2,1)}, u32[]{:S(2)}) copy-start(bf16[512,512]{1,0:T(8,128)(2,1)} %param.32) | copy-start | bytes 1572868
  124.7 16.2 %copy-start.12 = (f32[512]{0:T(512)S(1)}, f32[512]{0:T(512)}, u32[]{:S(2)}) copy-start(f32[512]{0:T(512)} %param.33) | copy-start | bytes 6148
  124.7 16.2 %copy-start.13 = (f32[512]{0:T(512)S(1)}, f32[512]{0:T(512)}, u32[]{:S(2)}) copy-start(f32[512]{0:T(512)} %param.31) | copy-start | bytes 6148
  127.2 13.5 %all-to-all-start.1 = ((bf16[4,160,512]{2,1,0:T(8,128)(2,1)}), bf16[4,160,512]{2,1,0:T(8,128)(2,1)S(1)}, u32[]{:S(2)}, u32[]{:S(2)}) async-start(bf16[4,160,512]{2,1,0:T(8,128)(2,1)} %broadcast_in_dim.10), calls=%async_computation.1 | async-start | bytes 1310720 | tf_op jit(solution)/shard_map/all_to_all | solution.py:35
where the time goes:
time: 144 us; the launch traced here: 142 us
  matrix products  55.5 us (39%)
  waiting for transfers between devices  43.3 us (30%)
  starting transfers between devices  20.1 us (14%)
  blocking collectives  10.9 us (8%)
  local copies, waits for them, and re-layouts  9.17 us (6%)
  other arithmetic  3.13 us (2%)
    dot_general x16, matrix products, one_block(): jnp.dot(onehot, table, preferred_element_type=jnp.float32)  40.7 us
    all_to_all x1, waiting for transfers between devices, joined_exchange(): tiles = lax.all_to_all(tiles, axis, split_axis=0, concat_axis=0, tiled=True)  35 us
    all_to_all x1, starting transfers between devices, joined_exchange(): tiles = lax.all_to_all(tiles, axis, split_axis=0, concat_axis=0, tiled=True)  16.6 us
    all_gather x1, blocking collectives, body(): portion = lax.all_gather(mesh_latent, 'feat', axis=1, tiled=True)  10.9 us
    all_to_all x1, waiting for transfers between devices, from_everyone(): lax.all_to_all(jnp.broadcast_to(value[None], (length, *value.shape)), axi...  8.27 us
    dot_general x1, matrix products, body(): jnp.dot(own_edges, edge_w1[:full_width], preferred_element_type=jnp.float32)  4.24 us
    unnamed x30, local copies, waits for them, and re-layouts  3.98 us
    all_to_all x1, starting transfers between devices, from_everyone(): lax.all_to_all(jnp.broadcast_to(value[None], (length, *value.shape)), axi...  3.48 us
  transfers between devices with their start and end apart: 2, of which 2 were waited for; matrix products, arithmetic and copies ran while one was open for 7% of the time, Pallas kernels for 0%

commit v1 on v0

--- a/solution.py
+++ b/solution.py
@@ -109,7 +109,13 @@
     own_edges = edge_latent.reshape(-1, full_width)
     targets = edge_dst.reshape(-1)
     recv_weight = edge_w1[2 * full_width :]
-    portion = lax.all_gather(mesh_latent, "feat", axis=1, tiled=True)
+    size = lax.axis_size("feat")
+    held, tiles_2 = (mesh_latent, [mesh_latent])
+    for _ in range(size - 1):
+        held = lax.ppermute(held, "feat", [(i, (i + 1) % size) for i in range(size)])
+        tiles_2.insert(0, held)
+    line = jnp.concatenate(tiles_2, axis=1)
+    portion = jnp.roll(line, (lax.axis_index("feat") + 1) * mesh_latent.shape[1], axis=1)
     projected = jnp.dot(portion, recv_weight, preferred_element_type=jnp.float32)
     node_ids = lax.broadcasted_iota(jnp.int32, (mesh_count, targets.shape[0]), 0)
     clipped = jnp.minimum(targets, mesh_count - 1)

time: 144 us -> 144 us (level)
  blocking collectives: 10.9 us -> 0 us
  waiting for transfers between devices: 43.3 us -> 52.1 us
  starting transfers between devices: 20.1 us -> 22.3 us
    all_gather x1 -> x0, blocking collectives: 10.9 us -> none  [body(): portion = lax.all_gather(mesh_latent, 'feat', axis=1, tiled=True)]
    ppermute x0 -> x3, waiting for transfers between devices: none -> 6.91 us  [body(): lax.ppermute(held, 'feat', [(i, (i + 1) % size) for i in range(size)])]
    ppermute x0 -> x3, starting transfers between devices: none -> 2.17 us  [body(): lax.ppermute(held, 'feat', [(i, (i + 1) % size) for i in range(size)])]
    all_to_all x1, waiting for transfers between devices: 35 us -> 36.6 us  [joined_exchange(): tiles = lax.all_to_all(tiles, axis, split_axis=0, concat_axis=0, tiled=True)]
    unnamed x30 -> x37, local copies, waits for them, and re-layouts: 3.98 us -> 4.05 us
  transfers between devices with their start and end apart: 2 -> 5, of which waited for: 2 -> 5; matrix products, arithmetic and copies ran while one was open for 7% -> 7% of each run, Pallas kernels for 0% -> 0%
where the time goes in v1:
time: 144 us; the launch traced here: 143 us
  matrix products  55.5 us (39%)
  waiting for transfers between devices  52.1 us (36%)
  starting transfers between devices  22.3 us (15%)
  local copies, waits for them, and re-layouts  9.25 us (6%)
  other arithmetic  3.08 us (2%)
    dot_general x16, matrix products, one_block(): jnp.dot(onehot, table, preferred_element_type=jnp.float32)  40.6 us
    all_to_all x1, waiting for transfers between devices, joined_exchange(): tiles = lax.all_to_all(tiles, axis, split_axis=0, concat_axis=0, tiled=True)  36.6 us
    all_to_all x1, starting transfers between devices, joined_exchange(): tiles = lax.all_to_all(tiles, axis, split_axis=0, concat_axis=0, tiled=True)  16.6 us
    all_to_all x1, waiting for transfers between devices, from_everyone(): lax.all_to_all(jnp.broadcast_to(value[None], (length, *value.shape)), axi...  8.54 us
    ppermute x3, waiting for transfers between devices, body(): lax.ppermute(held, 'feat', [(i, (i + 1) % size) for i in range(size)])  6.91 us
    dot_general x1, matrix products, body(): jnp.dot(own_edges, edge_w1[:full_width], preferred_element_type=jnp.float32)  4.23 us
    unnamed x37, local copies, waits for them, and re-layouts  4.05 us
    all_to_all x1, starting transfers between devices, from_everyone(): lax.all_to_all(jnp.broadcast_to(value[None], (length, *value.shape)), axi...  3.48 us
  transfers between devices with their start and end apart: 5, of which 5 were waited for; matrix products, arithmetic and copies ran while one was open for 7% of the time, Pallas kernels for 0%

profile of v1, /device:TPU:1, one launch (start us, length us, event | category | flops | bytes accessed | tf_op | source)
XLA Modules:
  0.0 142.6 jit_solution(1961370560749948848)
XLA Ops:
  0.5 1.4 reduce.4
  1.9 40.8 %while.10 = (s32[]{:T(128)}, bf16[16,512,128]{2,1,0:T(8,128)(2,1)}, s32[16,512]{1,0:T(8,128)S(1)}, bf16[2048,128]{1,0:T(8,128)(2,1)}, s32[]{:T(128)}) while((s32[]{:T(128)}, bf16[16,512,128]{2,1,0:T(8,128)(2,1)}, s32[16,512]{1,0:T(8,128)S(1)}, bf16[2048,128]{1,0:T(8,128)(2,1)}, s32[]{:T(128)}) %tuple.21), condition=%wide.region_1.2_spmd, body=%wide.region_0.1_spmd.sunk | while | flops 269549568 | bytes 662081 | solution.py:79
  1.9 2.5 %fusion.53 = bf16[16,512,128]{2,1,0:T(8,128)(2,1)} fusion(bf16[16,512,128]{2,1,0:T(8,128)(2,1)} %get-tuple-element.73, s32[]{:T(128)} %get-tuple-element.72, bf16[2048,128]{1,0:T(8,128)(2,1)} %get-tuple-element.80, s32[512]{0:T(512)S(1)} %bitcast.40), kind=kOutput, calls=%fused_computation.5.clone.1 | convolution fusion | flops 269549568 | bytes 657920 | tf_op jit(solution)/shard_map/while/body/eval_jaxpr/dot_general | solution.py:77
  4.5 2.5 %fusion.53 = bf16[16,512,128]{2,1,0:T(8,128)(2,1)} fusion(bf16[16,512,128]{2,1,0:T(8,128)(2,1)} %get-tuple-element.73, s32[]{:T(128)} %get-tuple-element.72, bf16[2048,128]{1,0:T(8,128)(2,1)} %get-tuple-element.80, s32[512]{0:T(512)S(1)} %bitcast.40), kind=kOutput, calls=%fused_computation.5.clone.1 | convolution fusion | flops 269549568 | bytes 657920 | tf_op jit(solution)/shard_map/while/body/eval_jaxpr/dot_general | solution.py:77
  7.1 2.5 %fusion.53 = bf16[16,512,128]{2,1,0:T(8,128)(2,1)} fusion(bf16[16,512,128]{2,1,0:T(8,128)(2,1)} %get-tuple-element.73, s32[]{:T(128)} %get-tuple-element.72, bf16[2048,128]{1,0:T(8,128)(2,1)} %get-tuple-element.80, s32[512]{0:T(512)S(1)} %bitcast.40), kind=kOutput, calls=%fused_computation.5.clone.1 | convolution fusion | flops 269549568 | bytes 657920 | tf_op jit(solution)/shard_map/while/body/eval_jaxpr/dot_general | solution.py:77
  9.6 2.5 %fusion.53 = bf16[16,512,128]{2,1,0:T(8,128)(2,1)} fusion(bf16[16,512,128]{2,1,0:T(8,128)(2,1)} %get-tuple-element.73, s32[]{:T(128)} %get-tuple-element.72, bf16[2048,128]{1,0:T(8,128)(2,1)} %get-tuple-element.80, s32[512]{0:T(512)S(1)} %bitcast.40), kind=kOutput, calls=%fused_computation.5.clone.1 | convolution fusion | flops 269549568 | bytes 657920 | tf_op jit(solution)/shard_map/while/body/eval_jaxpr/dot_general | solution.py:77
  12.1 2.5 %fusion.53 = bf16[16,512,128]{2,1,0:T(8,128)(2,1)} fusion(bf16[16,512,128]{2,1,0:T(8,128)(2,1)} %get-tuple-element.73, s32[]{:T(128)} %get-tuple-element.72, bf16[2048,128]{1,0:T(8,128)(2,1)} %get-tuple-element.80, s32[512]{0:T(512)S(1)} %bitcast.40), kind=kOutput, calls=%fused_computation.5.clone.1 | convolution fusion | flops 269549568 | bytes 657920 | tf_op jit(solution)/shard_map/while/body/eval_jaxpr/dot_general | solution.py:77
  14.7 2.5 %fusion.53 = bf16[16,512,128]{2,1,0:T(8,128)(2,1)} fusion(bf16[16,512,128]{2,1,0:T(8,128)(2,1)} %get-tuple-element.73, s32[]{:T(128)} %get-tuple-element.72, bf16[2048,128]{1,0:T(8,128)(2,1)} %get-tuple-element.80, s32[512]{0:T(512)S(1)} %bitcast.40), kind=kOutput, calls=%fused_computation.5.clone.1 | convolution fusion | flops 269549568 | bytes 657920 | tf_op jit(solution)/shard_map/while/body/eval_jaxpr/dot_general | solution.py:77
  17.2 2.5 %fusion.53 = bf16[16,512,128]{2,1,0:T(8,128)(2,1)} fusion(bf16[16,512,128]{2,1,0:T(8,128)(2,1)} %get-tuple-element.73, s32[]{:T(128)} %get-tuple-element.72, bf16[2048,128]{1,0:T(8,128)(2,1)} %get-tuple-element.80, s32[512]{0:T(512)S(1)} %bitcast.40), kind=kOutput, calls=%fused_computation.5.clone.1 | convolution fusion | flops 269549568 | bytes 657920 | tf_op jit(solution)/shard_map/while/body/eval_jaxpr/dot_general | solution.py:77
  19.8 2.5 %fusion.53 = bf16[16,512,128]{2,1,0:T(8,128)(2,1)} fusion(bf16[16,512,128]{2,1,0:T(8,128)(2,1)} %get-tuple-element.73, s32[]{:T(128)} %get-tuple-element.72, bf16[2048,128]{1,0:T(8,128)(2,1)} %get-tuple-element.80, s32[512]{0:T(512)S(1)} %bitcast.40), kind=kOutput, calls=%fused_computation.5.clone.1 | convolution fusion | flops 269549568 | bytes 657920 | tf_op jit(solution)/shard_map/while/body/eval_jaxpr/dot_general | solution.py:77
  22.3 2.5 %fusion.53 = bf16[16,512,128]{2,1,0:T(8,128)(2,1)} fusion(bf16[16,512,128]{2,1,0:T(8,128)(2,1)} %get-tuple-element.73, s32[]{:T(128)} %get-tuple-element.72, bf16[2048,128]{1,0:T(8,128)(2,1)} %get-tuple-element.80, s32[512]{0:T(512)S(1)} %bitcast.40), kind=kOutput, calls=%fused_computation.5.clone.1 | convolution fusion | flops 269549568 | bytes 657920 | tf_op jit(solution)/shard_map/while/body/eval_jaxpr/dot_general | solution.py:77
  24.9 2.5 %fusion.53 = bf16[16,512,128]{2,1,0:T(8,128)(2,1)} fusion(bf16[16,512,128]{2,1,0:T(8,128)(2,1)} %get-tuple-element.73, s32[]{:T(128)} %get-tuple-element.72, bf16[2048,128]{1,0:T(8,128)(2,1)} %get-tuple-element.80, s32[512]{0:T(512)S(1)} %bitcast.40), kind=kOutput, calls=%fused_computation.5.clone.1 | convolution fusion | flops 269549568 | bytes 657920 | tf_op jit(solution)/shard_map/while/body/eval_jaxpr/dot_general | solution.py:77
  27.4 2.5 %fusion.53 = bf16[16,512,128]{2,1,0:T(8,128)(2,1)} fusion(bf16[16,512,128]{2,1,0:T(8,128)(2,1)} %get-tuple-element.73, s32[]{:T(128)} %get-tuple-element.72, bf16[2048,128]{1,0:T(8,128)(2,1)} %get-tuple-element.80, s32[512]{0:T(512)S(1)} %bitcast.40), kind=kOutput, calls=%fused_computation.5.clone.1 | convolution fusion | flops 269549568 | bytes 657920 | tf_op jit(solution)/shard_map/while/body/eval_jaxpr/dot_general | solution.py:77
  30.0 2.5 %fusion.53 = bf16[16,512,128]{2,1,0:T(8,128)(2,1)} fusion(bf16[16,512,128]{2,1,0:T(8,128)(2,1)} %get-tuple-element.73, s32[]{:T(128)} %get-tuple-element.72, bf16[2048,128]{1,0:T(8,128)(2,1)} %get-tuple-element.80, s32[512]{0:T(512)S(1)} %bitcast.40), kind=kOutput, calls=%fused_computation.5.clone.1 | convolution fusion | flops 269549568 | bytes 657920 | tf_op jit(solution)/shard_map/while/body/eval_jaxpr/dot_general | solution.py:77
  32.5 2.5 %fusion.53 = bf16[16,512,128]{2,1,0:T(8,128)(2,1)} fusion(bf16[16,512,128]{2,1,0:T(8,128)(2,1)} %get-tuple-element.73, s32[]{:T(128)} %get-tuple-element.72, bf16[2048,128]{1,0:T(8,128)(2,1)} %get-tuple-element.80, s32[512]{0:T(512)S(1)} %bitcast.40), kind=kOutput, calls=%fused_computation.5.clone.1 | convolution fusion | flops 269549568 | bytes 657920 | tf_op jit(solution)/shard_map/while/body/eval_jaxpr/dot_general | solution.py:77
  35.0 2.5 %fusion.53 = bf16[16,512,128]{2,1,0:T(8,128)(2,1)} fusion(bf16[16,512,128]{2,1,0:T(8,128)(2,1)} %get-tuple-element.73, s32[]{:T(128)} %get-tuple-element.72, bf16[2048,128]{1,0:T(8,128)(2,1)} %get-tuple-element.80, s32[512]{0:T(512)S(1)} %bitcast.40), kind=kOutput, calls=%fused_computation.5.clone.1 | convolution fusion | flops 269549568 | bytes 657920 | tf_op jit(solution)/shard_map/while/body/eval_jaxpr/dot_general | solution.py:77
  37.6 2.6 %fusion.53 = bf16[16,512,128]{2,1,0:T(8,128)(2,1)} fusion(bf16[16,512,128]{2,1,0:T(8,128)(2,1)} %get-tuple-element.73, s32[]{:T(128)} %get-tuple-element.72, bf16[2048,128]{1,0:T(8,128)(2,1)} %get-tuple-element.80, s32[512]{0:T(512)S(1)} %bitcast.40), kind=kOutput, calls=%fused_computation.5.clone.1 | convolution fusion | flops 269549568 | bytes 657920 | tf_op jit(solution)/shard_map/while/body/eval_jaxpr/dot_general | solution.py:77
  40.1 2.5 %fusion.53 = bf16[16,512,128]{2,1,0:T(8,128)(2,1)} fusion(bf16[16,512,128]{2,1,0:T(8,128)(2,1)} %get-tuple-element.73, s32[]{:T(128)} %get-tuple-element.72, bf16[2048,128]{1,0:T(8,128)(2,1)} %get-tuple-element.80, s32[512]{0:T(512)S(1)} %bitcast.40), kind=kOutput, calls=%fused_computation.5.clone.1 | convolution fusion | flops 269549568 | bytes 657920 | tf_op jit(solution)/shard_map/while/body/eval_jaxpr/dot_general | solution.py:77
  42.7 16.6 %all-to-all-start = ((bf16[256,1,32,128]{3,2,1,0:T(8,128)(2,1)}), bf16[256,1,32,128]{3,2,1,0:T(8,128)(2,1)}, u32[]{:S(2)}, u32[]{:S(2)}) async-start(bf16[256,1,32,128]{3,2,1,0:T(8,128)(2,1)} %bitcast.4), calls=%async_computation | async-start | bytes 4194304 | tf_op jit(solution)/shard_map/all_to_all | solution.py:28
  59.4 1.4 %collective-permute-start = (bf16[160,128]{1,0:T(8,128)(2,1)S(1)}, bf16[160,128]{1,0:T(8,128)(2,1)S(1)}, u32[]{:S(2)}, u32[]{:S(2)}) collective-permute-start(bf16[160,128]{1,0:T(8,128)(2,1)S(1)} %copy-done.5), channel_id=1, source_target_pairs={{0,1},{1,2},{2,3},{3,0},{4,5},{5,6},{6,7},{7,4},{8,9},{9,10},{10,1... | collective-permute-start | bytes 122888 | tf_op jit(solution)/shard_map/ppermute | solution.py:115
  60.8 4.1 %collective-permute-done = bf16[160,128]{1,0:T(8,128)(2,1)S(1)} collective-permute-done((bf16[160,128]{1,0:T(8,128)(2,1)S(1)}, bf16[160,128]{1,0:T(8,128)(2,1)S(1)}, u32[]{:S(2)}, u32[]{:S(2)}) %collective-permute-start) | collective-permute-done | bytes 40992 | tf_op jit(solution)/shard_map/ppermute | solution.py:115
  65.1 4.2 %fusion.8 = f32[2048,512]{1,0:T(8,128)} fusion(bf16[1,1,2048,512]{3,2,1,0:T(8,128)(2,1)S(1)} %copy-done.1, bf16[1536,512]{1,0:T(8,128)(2,1)} %param.24), kind=kOutput, calls=%fused_computation.14 | convolution fusion | flops 1073741824 | bytes 6815744 | tf_op jit(solution)/shard_map/dot_general | solution.py:130
  70.5 2.5 %copy.24 = bf16[1,1,2048,512]{2,3,1,0:T(8,128)(2,1)} copy(bf16[1,1,2048,512]{3,2,1,0:T(8,128)(2,1)S(1)} %copy-done.1) | data formatting | bytes 4194304 | tf_op args[2]
  73.0 2.2 %collective-permute-done.2 = bf16[160,128]{1,0:T(8,128)(2,1)S(1)} collective-permute-done((bf16[160,128]{1,0:T(8,128)(2,1)S(1)}, bf16[160,128]{1,0:T(8,128)(2,1)S(1)}, u32[]{:S(2)}, u32[]{:S(2)}) %collective-permute-start.2) | collective-permute-done | bytes 40992 | tf_op jit(solution)/shard_map/ppermute | solution.py:115
  76.7 36.6 %all-to-all-done = bf16[256,1,32,128]{3,2,1,0:T(8,128)(2,1)} async-done(((bf16[256,1,32,128]{3,2,1,0:T(8,128)(2,1)}), bf16[256,1,32,128]{3,2,1,0:T(8,128)(2,1)}, u32[]{:S(2)}, u32[]{:S(2)}) %all-to-all-start) | async-done | bytes 2097184 | tf_op jit(solution)/shard_map/all_to_all | solution.py:28
  113.3 2.7 %copy.25 = bf16[64,32,4,128]{3,2,1,0:T(4,128)(2,1)S(1)} copy(bf16[64,32,4,128]{3,1,2,0:T(8,128)(2,1)} %bitcast.8) | data formatting | bytes 4194304 | tf_op jit(solution)/shard_map/transpose | solution.py:17
  116.0 2.5 %fusion.5 = f32[2048,512]{1,0:T(8,128)S(1)} fusion(bf16[256,8,4,128]{3,2,1,0:T(4,128)(2,1)S(1)} %bitcast.39, bf16[1536,512]{1,0:T(8,128)(2,1)} %param.24), kind=kOutput, calls=%fused_computation.11 | convolution fusion | flops 1073741824 | bytes 6815744 | tf_op jit(solution)/shard_map/dot_general | solution.py:131
  118.5 3.0 %multiply_convert_fusion = bf16[2048,512]{1,0:T(8,128)(2,1)S(1)} fusion(f32[2048,512]{1,0:T(8,128)S(1)} %copy-done.2, f32[2048,512]{1,0:T(8,128)S(1)} %fusion.5, f32[160,512]{1,0:T(8,128)S(1)} %fusion.17, f32[512]{0:T(512)S(1)} %copy-done.9, s32[2048]{0:T(1024)S(1)} %broadcast_minimum_fusion), kind=kOutput, calls=%fused_computation.9 | convolution fusion | flops 2021982208 | bytes 10823680 | tf_op jit(solution)/shard_map/dot_general | solution.py:123
  121.5 1.4 add_reduce_fusion
  124.5 1.6 %fusion.12 = bf16[160,512]{1,0:T(8,128)(2,1)S(1)} fusion(f32[2048,512]{0,1:T(8,128)S(1)} %get-tuple-element.39, bf16[1,1,2048,512]{2,3,1,0:T(8,128)(2,1)S(1)} %copy-done.3, f32[512]{0:T(512)S(1)} %copy-done.10, f32[512]{0:T(512)S(1)} %copy-done.11, f32[2048]{0:T(1024)S(1)} %add_rsqrt_fusion, f32[2048]{0:T(1024)S(1)} %broadcast_multiply_fusion, ...), kind=kOutput, calls=%fused_computation.22 | convolution fusion | flops 344342528 | bytes 6486016 | tf_op jit(solution)/shard_map/dot_general | solution.py:141
  127.1 3.5 %all-to-all-start.1 = ((bf16[4,160,512]{2,1,0:T(8,128)(2,1)}), bf16[4,160,512]{2,1,0:T(8,128)(2,1)S(1)}, u32[]{:S(2)}, u32[]{:S(2)}) async-start(bf16[4,160,512]{2,1,0:T(8,128)(2,1)} %broadcast_in_dim.10), calls=%async_computation.1 | async-start | bytes 1310720 | tf_op jit(solution)/shard_map/all_to_all | solution.py:35
  132.1 8.5 %all-to-all-done.1 = bf16[4,160,512]{2,1,0:T(8,128)(2,1)S(1)} async-done(((bf16[4,160,512]{2,1,0:T(8,128)(2,1)}), bf16[4,160,512]{2,1,0:T(8,128)(2,1)S(1)}, u32[]{:S(2)}, u32[]{:S(2)}) %all-to-all-start.1) | async-done | bytes 655392 | tf_op jit(solution)/shard_map/all_to_all | solution.py:35
  (73 shorter events, 9.4 us)
Async XLA Ops:
  0.0 121.5 %copy-start = (bf16[512,512]{1,0:T(8,128)(2,1)S(1)}, bf16[512,512]{1,0:T(8,128)(2,1)}, u32[]{:S(2)}) copy-start(bf16[512,512]{1,0:T(8,128)(2,1)} %param.26) | copy-start | bytes 1572868
  42.7 16.7 %copy-start.5 = (bf16[160,128]{1,0:T(8,128)(2,1)S(1)}, bf16[160,128]{1,0:T(8,128)(2,1)}, u32[]{:S(2)}) copy-start(bf16[160,128]{1,0:T(8,128)(2,1)} %param.20) | copy-start | bytes 122884
  42.7 22.4 %copy-start.1 = (bf16[1,1,2048,512]{3,2,1,0:T(8,128)(2,1)S(1)}, bf16[1,1,2048,512]{3,2,1,0:T(8,128)(2,1)}, u32[]{:S(2)}) copy-start(bf16[1,1,2048,512]{3,2,1,0:T(8,128)(2,1)} %param.21) | copy-start | bytes 6291460
  42.7 70.6 %all-to-all-start = ((bf16[256,1,32,128]{3,2,1,0:T(8,128)(2,1)}), bf16[256,1,32,128]{3,2,1,0:T(8,128)(2,1)}, u32[]{:S(2)}, u32[]{:S(2)}) async-start(bf16[256,1,32,128]{3,2,1,0:T(8,128)(2,1)} %bitcast.4), calls=%async_computation | async-start | bytes 4194304 | tf_op jit(solution)/shard_map/all_to_all | solution.py:28
  59.4 11.1 %copy-start.6 = (s32[1,1,2048]{2,1,0:T(1,128)S(1)}, s32[1,1,2048]{2,1,0:T(1,128)}, u32[]{:S(2)}) copy-start(s32[1,1,2048]{2,1,0:T(1,128)} %param.23) | copy-start | bytes 24580
  59.4 5.5 %collective-permute-start = (bf16[160,128]{1,0:T(8,128)(2,1)S(1)}, bf16[160,128]{1,0:T(8,128)(2,1)S(1)}, u32[]{:S(2)}, u32[]{:S(2)}) collective-permute-start(bf16[160,128]{1,0:T(8,128)(2,1)S(1)} %copy-done.5), channel_id=1, source_target_pairs={{0,1},{1,2},{2,3},{3,0},{4,5},{5,6},{6,7},{7,4},{8,9},{9,10},{10,1... | collective-permute-start | bytes 122888 | tf_op jit(solution)/shard_map/ppermute | solution.py:115
  64.9 5.1 %collective-permute-start.1 = (bf16[160,128]{1,0:T(8,128)(2,1)S(1)}, bf16[160,128]{1,0:T(8,128)(2,1)S(1)}, u32[]{:S(2)}, u32[]{:S(2)}) collective-permute-start(bf16[160,128]{1,0:T(8,128)(2,1)S(1)} %collective-permute-done), channel_id=1, source_target_pairs={{0,1},{1,2},{2,3},{3,0},{4,5},{5,6},{6,7},{7,4},{8,9},{9,10},{10,1... | collective-permute-start | bytes 122888 | tf_op jit(solution)/shard_map/ppermute | solution.py:115
  69.9 5.2 %collective-permute-start.2 = (bf16[160,128]{1,0:T(8,128)(2,1)S(1)}, bf16[160,128]{1,0:T(8,128)(2,1)S(1)}, u32[]{:S(2)}, u32[]{:S(2)}) collective-permute-start(bf16[160,128]{1,0:T(8,128)(2,1)S(1)} %collective-permute-done.1), channel_id=1, source_target_pairs={{0,1},{1,2},{2,3},{3,0},{4,5},{5,6},{6,7},{7,4},{8,9},{9,10},{10,1... | collective-permute-start | bytes 122888 | tf_op jit(solution)/shard_map/ppermute | solution.py:115
  116.0 2.5 %copy-start.2 = (f32[2048,512]{1,0:T(8,128)S(1)}, f32[2048,512]{1,0:T(8,128)}, u32[]{:S(2)}) copy-start(f32[2048,512]{1,0:T(8,128)} %fusion.8) | copy-start | bytes 12582916
  116.0 2.5 %copy-start.9 = (f32[512]{0:T(512)S(1)}, f32[512]{0:T(512)}, u32[]{:S(2)}) copy-start(f32[512]{0:T(512)} %param.25) | copy-start | bytes 6148
  118.5 3.0 %copy-start.7 = (f32[512]{0:T(512)S(1)}, f32[512]{0:T(512)}, u32[]{:S(2)}) copy-start(f32[512]{0:T(512)} %param.27) | copy-start | bytes 6148
  122.9 1.6 %copy-start.3 = (bf16[1,1,2048,512]{2,3,1,0:T(8,128)(2,1)S(1)}, bf16[1,1,2048,512]{2,3,1,0:T(8,128)(2,1)}, u32[]{:S(2)}) copy-start(bf16[1,1,2048,512]{2,3,1,0:T(8,128)(2,1)} %copy.24) | copy-start | bytes 6291460
  122.9 1.6 %copy-start.10 = (f32[512]{0:T(512)S(1)}, f32[512]{0:T(512)}, u32[]{:S(2)}) copy-start(f32[512]{0:T(512)} %param.29) | copy-start | bytes 6148
  122.9 1.6 %copy-start.11 = (f32[512]{0:T(512)S(1)}, f32[512]{0:T(512)}, u32[]{:S(2)}) copy-start(f32[512]{0:T(512)} %param.28) | copy-start | bytes 6148
  124.5 16.2 %copy-start.4 = (bf16[1024,512]{1,0:T(8,128)(2,1)S(1)}, bf16[1024,512]{1,0:T(8,128)(2,1)}, u32[]{:S(2)}) copy-start(bf16[1024,512]{1,0:T(8,128)(2,1)} %param.30) | copy-start | bytes 3145732
  124.5 16.4 %copy-start.8 = (bf16[512,512]{1,0:T(8,128)(2,1)S(1)}, bf16[512,512]{1,0:T(8,128)(2,1)}, u32[]{:S(2)}) copy-start(bf16[512,512]{1,0:T(8,128)(2,1)} %param.32) | copy-start | bytes 1572868
  124.5 16.5 %copy-start.12 = (f32[512]{0:T(512)S(1)}, f32[512]{0:T(512)}, u32[]{:S(2)}) copy-start(f32[512]{0:T(512)} %param.33) | copy-start | bytes 6148
  124.5 16.4 %copy-start.13 = (f32[512]{0:T(512)S(1)}, f32[512]{0:T(512)}, u32[]{:S(2)}) copy-start(f32[512]{0:T(512)} %param.31) | copy-start | bytes 6148
  127.1 13.5 %all-to-all-start.1 = ((bf16[4,160,512]{2,1,0:T(8,128)(2,1)}), bf16[4,160,512]{2,1,0:T(8,128)(2,1)S(1)}, u32[]{:S(2)}, u32[]{:S(2)}) async-start(bf16[4,160,512]{2,1,0:T(8,128)(2,1)} %broadcast_in_dim.10), calls=%async_computation.1 | async-start | bytes 1310720 | tf_op jit(solution)/shard_map/all_to_all | solution.py:35
